TPU v7x, 128 devices: a whole 4x4x4 slice. The times are simulated.
128 devices in a mesh: section: 8 (over z, x_lo), dp: 16 (over x_hi, y, core).
Axes of the slice: x: 4 (x_hi: 2, x_lo: 2; x = x_hi * 2 + x_lo), y: 4, z: 4, core: 2. Of those that a mesh axis runs over, the one named last changes fastest.
Arguments:
- acts: bfloat16 [8, 6144, 8192], P('section', 'dp'), may hold values from -6 to 6
- input_grads: bfloat16 [8, 6144, 5120], P('section', 'dp'), may hold values from -6 to 6
- head_grads: bfloat16 [6144, 5120], P('dp'), may hold values from -6 to 6
- weight_grad: bfloat16 [8, 5120, 8192], P('section', None, 'dp'), may hold values from -6 to 6
- sweeps: int32 [8, 52], P('section'), may hold values from 1 to 4
Outputs:
- update: bfloat16 [8, 5120, 8192], P('section', None, 'dp')
Inputs may be any that keep to these rules, and one draw needn't show every extreme that they name: sweeps[s, k] is the number of Newton-Schulz iterations of block k of layer s; every value from 1 to 4 occurs.
All inputs are finite; a program needn't handle non-finite values. Where the computation divides by a largest or mean magnitude, that divisor is 1e-20 or more.
Results may differ from a plain program's by a relative error of at most 0.0067.
Values may be sent and summed in bfloat16 or wider, within the bound.
A program may use at most 128 MiB of HBM per device.

v0:
```python
import jax
import jax.numpy as jnp
from jax import lax
from jax.sharding import PartitionSpec as P

BLOCK = 256


damping = 0.05


def passed_along(block, axis, distance):
    devices = range(lax.axis_size(axis))
    route = [(i - distance, i) for i in devices if i - distance in devices]
    return lax.ppermute(block, axis, route)


def newton_single(matrix, count):
    eye = jnp.eye(matrix.shape[0], dtype=jnp.float32)
    scale = 1.0 / jnp.max(jnp.sum(jnp.abs(matrix), axis=1))

    def sweep(turn, approx):
        inner = 2.0 * eye - jnp.dot(matrix, approx, precision=lax.Precision.HIGHEST)
        return jnp.dot(approx, inner, precision=lax.Precision.HIGHEST)

    return lax.fori_loop(0, count, sweep, scale * eye)


def on_device(acts, input_grads, head_grads, weight_grad, sweeps):
    dp_count = lax.axis_size("dp")
    owner_index = lax.axis_index("dp")
    section_count = lax.axis_size("section")
    section_index = lax.axis_index("section")
    arrived = passed_along(input_grads, "section", -1)
    grads = jnp.where(section_index == section_count - 1, head_grads[None], arrived)[0]
    inputs = acts[0]
    tokens_here = inputs.shape[0]
    hidden_blocks = inputs.shape[1] // BLOCK
    model_blocks = grads.shape[1] // BLOCK
    shaped_a = inputs.reshape(tokens_here, hidden_blocks, BLOCK)
    shaped_g = grads.reshape(tokens_here, model_blocks, BLOCK)
    part_a = jnp.einsum("tkb,tkc->kbc", shaped_a, shaped_a, preferred_element_type=jnp.float32)
    part_g = jnp.einsum("tkb,tkc->kbc", shaped_g, shaped_g, preferred_element_type=jnp.float32)
    partial_value = jnp.concatenate([part_a, part_g], axis=0)
    block_count = partial_value.shape[0]
    capacity = -(-block_count // dp_count)
    slot_total = dp_count * capacity
    counts = sweeps[0]
    block_ids = jnp.arange(block_count, dtype=jnp.int32)
    ordering = jnp.argsort(-counts, stable=True)
    rank_of = jnp.argsort(ordering, stable=True)
    rounds = rank_of // dp_count
    within = rank_of % dp_count
    owner_of = jnp.where(rounds % 2 == 0, within, dp_count - 1 - within)
    slot_of = owner_of * capacity + rounds
    slot_ids = jnp.arange(slot_total, dtype=jnp.int32)
    matches = slot_of[None, :] == slot_ids[:, None]
    block_of = jnp.sum(jnp.where(matches, block_ids[None, :] + 1, 0), axis=1) - 1
    block_of = jnp.where(block_of < 0, block_count, block_of)
    my_blocks = lax.dynamic_slice_in_dim(block_of, owner_index * capacity, capacity)
    zero_block = jnp.zeros((1, BLOCK, BLOCK), jnp.float32)
    outgoing = jnp.take(jnp.concatenate([partial_value, zero_block], axis=0), block_of, axis=0)
    mine = lax.psum_scatter(outgoing, "dp", scatter_dimension=0, tiled=True)
    eye = jnp.eye(BLOCK, dtype=jnp.float32)
    factor = mine / (tokens_here * dp_count) + damping * eye[None]
    padded_counts = jnp.concatenate([counts, jnp.zeros((1,), jnp.int32)])
    my_counts = jnp.take(padded_counts, my_blocks)
    inverted = []
    for position in range(capacity):
        inverted.append(newton_single(factor[position], my_counts[position]))
    inverse = jnp.stack(inverted).astype(jnp.bfloat16)
    every_inverse = lax.all_gather(inverse, "dp", axis=0, tiled=True)
    column_count = weight_grad.shape[2]
    local_blocks = column_count // BLOCK
    column_blocks = owner_index * local_blocks + jnp.arange(local_blocks, dtype=jnp.int32)
    inverse_a = jnp.take(every_inverse, jnp.take(slot_of, column_blocks), axis=0)
    inverse_g = jnp.take(every_inverse, slot_of[hidden_blocks:], axis=0)
    weights = weight_grad[0].reshape(grads.shape[1], local_blocks, BLOCK)
    half = jnp.einsum(
        "dkb,kbc->dkc", weights, inverse_a, preferred_element_type=jnp.float32
    ).astype(jnp.bfloat16)
    half = half.reshape(model_blocks, BLOCK, column_count)
    update = jnp.einsum("kab,kbc->kac", inverse_g, half, preferred_element_type=jnp.float32)
    return update.reshape(grads.shape[1], column_count).astype(jnp.bfloat16)[None]


def solution(mesh):
    return jax.shard_map(
        on_device,
        mesh=mesh,
        in_specs=(
            P("section", "dp", None),
            P("section", "dp", None),
            P("dp", None),
            P("section", None, "dp"),
            P("section", None),
        ),
        out_specs=P("section", None, "dp"),
        check_vma=False,
    )
```

profile of v0, /device:TPU:1, one launch (start us, length us, event | category | flops | bytes accessed | tf_op | source)
XLA Modules:
  0.0 424.2 jit_solution(5902779405749802226)
XLA Ops:
  6.5 6.3 %copy.39 = bf16[1,384,5120]{1,2,0:T(8,128)(2,1)} copy(bf16[1,384,5120]{2,1,0:T(8,128)(2,1)} %param.14) | data formatting | bytes 7864320 | tf_op args[1]
  12.8 1.3 collective-permute-start
  14.1 6.3 %copy.38 = bf16[384,5120]{0,1:T(8,128)(2,1)} copy(bf16[384,5120]{1,0:T(8,128)(2,1)} %param.15) | data formatting | bytes 7864320 | tf_op args[2]
  20.4 7.6 %copy.52 = bf16[48,8,32,256]{3,2,1,0:T(8,128)(2,1)} copy(bf16[48,8,32,256]{3,1,2,0:T(8,128)(2,1)} %bitcast.126) | data formatting | bytes 12582912
  28.0 2.1 sort.31
  30.1 2.1 sort.32
  32.4 18.6 %fusion.9 = f32[32,256,256]{2,1,0:T(8,128)S(1)} fusion(bf16[384,32,256]{2,1,0:T(8,128)(2,1)} %bitcast.125), kind=kOutput, calls=%fused_computation.25 | convolution fusion | flops 1610612736 | bytes 14680064 | tf_op jit(solution)/shard_map/tkb,tkc->kbc/dot_general | solution.py:42
  51.0 50.3 %collective-permute-done = bf16[1,384,5120]{1,2,0:T(8,128)(2,1)} collective-permute-done((bf16[1,384,5120]{1,2,0:T(8,128)(2,1)}, bf16[1,384,5120]{1,2,0:T(8,128)(2,1)}, u32[]{:S(2)}, u32[]{:S(2)}) %collective-permute-start) | collective-permute-done | bytes 3932192 | tf_op jit(solution)/shard_map/ppermute | solution.py:15
  101.3 3.8 bitcast_select_fusion
  105.1 1.5 fusion.35
  106.6 5.2 %maximum_maximum_fusion = f32[53,256,256]{2,1,0:T(8,128)} fusion(f32[20,256,256]{2,1,0:T(8,128)S(1)} %fusion.35, f32[32,256,256]{2,1,0:T(8,128)S(1)} %fusion.9, f32[53]{0:T(128)S(1)} %pad.8.clone), kind=kLoop, calls=%fused_computation.21 | loop fusion | flops 6946816 | bytes 27525332 | tf_op jit(solution)/shard_map/concatenate | solution.py:62
  111.8 13.7 %gather_fusion = f32[64,256,256]{2,1,0:T(8,128)} fusion(f32[53,256,256]{2,1,0:T(8,128)} %maximum_maximum_fusion, s32[1024]{0:T(1024)S(1)} %pad_clamp_fusion.4), kind=kCustom, calls=%fused_computation | custom fusion | bytes 33554688 | tf_op jit(solution)/shard_map/jit(_take)/gather | solution.py:62
  125.5 11.6 %broadcast_select_fusion = f32[64,256,256]{2,1,0:T(8,128)} fusion(f32[64,256,256]{2,1,0:T(8,128)} %gather_fusion, pred[64]{0:T(512)(128)(4,1)S(1)} %compare_and_fusion.1), kind=kLoop, calls=%fused_computation.22 | loop fusion | flops 4194304 | bytes 33554496 | tf_op jit(solution)/shard_map/jit(_take)/select_n | solution.py:62
  138.2 0.7 fusion.34
  138.9 148.8 %reduce-scatter.2.cloned.1.call-done = f32[4,256,256]{2,1,0:T(8,128)} async-done(((f32[64,256,256]{2,1,0:T(8,128)}), f32[4,256,256]{2,1,0:T(8,128)}) %reduce-scatter.2.cloned.1.call-update) | async-done | bytes 1048592 | tf_op jit(solution)/shard_map/reduce_scatter | solution.py:63
  287.7 1.3 multiply_add_fusion
  289.3 0.7 reduce_max.36
  290.8 7.0 %while.44 = (s32[]{:T(128)}, f32[256,256]{0,1:T(8,128)S(1)}, s32[]{:T(128)}, f32[256,256]{1,0:T(8,128)S(1)}, s32[]{:T(128)}) while((s32[]{:T(128)}, f32[256,256]{0,1:T(8,128)S(1)}, s32[]{:T(128)}, f32[256,256]{1,0:T(8,128)S(1)}, s32[]{:T(128)}) %tuple.89), condition=%wide.region_7.8_spmd.clone, body=%wide.region_6.7_spmd.clone.sunk | while | flops 402849792 | bytes 2097213 | solution.py:26
  297.9 0.7 reduce_max.37
  299.4 5.7 %while.45 = (s32[]{:T(128)}, f32[256,256]{0,1:T(8,128)S(1)}, s32[]{:T(128)}, f32[256,256]{1,0:T(8,128)S(1)}, s32[]{:T(128)}) while((s32[]{:T(128)}, f32[256,256]{0,1:T(8,128)S(1)}, s32[]{:T(128)}, f32[256,256]{1,0:T(8,128)S(1)}, s32[]{:T(128)}) %tuple.86), condition=%wide.region_11.12_spmd.clone, body=%wide.region_10.11_spmd.clone.sunk | while | flops 402849792 | bytes 2097213 | solution.py:26
  305.2 0.7 reduce_max.38
  306.6 4.4 %while.46 = (s32[]{:T(128)}, f32[256,256]{0,1:T(8,128)S(1)}, s32[]{:T(128)}, f32[256,256]{1,0:T(8,128)S(1)}, s32[]{:T(128)}) while((s32[]{:T(128)}, f32[256,256]{0,1:T(8,128)S(1)}, s32[]{:T(128)}, f32[256,256]{1,0:T(8,128)S(1)}, s32[]{:T(128)}) %tuple.83), condition=%wide.region_15.16_spmd.clone, body=%wide.region_14.15_spmd.clone.sunk | while | flops 402849792 | bytes 2097213 | solution.py:26
  311.2 0.7 reduce_max.39
  313.3 0.9 pad_maximum_fusion
  314.3 0.6 gather_fusion.3
  314.9 8.3 %reshape_squeeze.11 = bf16[5120,2,256]{2,1,0:T(2,128)(2,1)} reshape(bf16[1,5120,512]{2,1,0:T(8,128)(2,1)} %param.16) | data formatting | bytes 10485760 | tf_op jit(solution)/shard_map/reshape;squeeze | solution.py:78
  323.4 62.3 %all-gather.2.cloned.1.call-done = bf16[64,256,256]{2,1,0:T(8,128)(2,1)} async-done(((bf16[4,256,256]{2,1,0:T(8,128)(2,1)}), bf16[64,256,256]{2,1,0:T(8,128)(2,1)}) %all-gather.2.cloned.1.call-update) | async-done | bytes 8388624 | tf_op jit(solution)/shard_map/all_gather | solution.py:72
  385.7 3.9 gather_fusion.4
  389.6 6.5 %fusion.8 = bf16[5120,2,256]{0,2,1:T(8,128)(2,1)} fusion(bf16[5120,2,256]{2,1,0:T(2,128)(2,1)} %reshape_squeeze.11, bf16[2,256,256]{2,1,0:T(8,128)(2,1)S(1)} %gather_fusion.4, pred[2]{0:T(512)(128)(4,1)S(1)} %compare_and_fusion), kind=kOutput, calls=%fused_computation.24 | convolution fusion | flops 1344929792 | bytes 10747906 | tf_op jit(solution)/shard_map/dkb,kbc->dkc/dot_general | solution.py:79
  396.1 10.0 %reshape.165 = bf16[20,256,512]{1,0,2:T(8,128)(2,1)} reshape(bf16[5120,2,256]{0,2,1:T(8,128)(2,1)} %fusion.8) | data formatting | bytes 10485760 | tf_op jit(solution)/shard_map/reshape | solution.py:82
  406.1 4.1 gather_fusion.2
  410.2 7.2 %fusion.14 = bf16[20,256,512]{2,1,0:T(8,128)(2,1)} fusion(bf16[20,256,512]{1,0,2:T(8,128)(2,1)} %reshape.165, bf16[20,256,256]{2,1,0:T(8,128)(2,1)S(1)} %gather_fusion.2, pred[20]{0:T(512)(128)(4,1)S(1)} %get-tuple-element.205), kind=kOutput, calls=%fused_computation.31 | convolution fusion | flops 1346109440 | bytes 13107220 | tf_op jit(solution)/shard_map/kab,kbc->kac/dot_general | solution.py:83
  (68 shorter events, 12.0 us)
Async XLA Ops:
  6.5 281.1 %reduce-scatter.2.cloned.1.call-start = ((), (), s32[]{:S(2)}) async-start(), calls=%async_computation.1 | async-start | bytes 17825792 | tf_op jit(solution)/shard_map/reduce_scatter | solution.py:63
  12.8 88.5 %collective-permute-start = (bf16[1,384,5120]{1,2,0:T(8,128)(2,1)}, bf16[1,384,5120]{1,2,0:T(8,128)(2,1)}, u32[]{:S(2)}, u32[]{:S(2)}) collective-permute-start(bf16[1,384,5120]{1,2,0:T(8,128)(2,1)} %copy.39), channel_id=1, source_target_pairs={{16,0},{32,16},{48,32},{64,48},{80,64},{96,80},{112,96},{17,1},{33... | collective-permute-start | bytes 11796488 | tf_op jit(solution)/shard_map/ppermute | solution.py:15
  20.4 7.6 %copy-start = (s32[1,52]{1,0:T(1,128)S(1)}, s32[1,52]{1,0:T(1,128)}, u32[]{:S(2)}) copy-start(s32[1,52]{1,0:T(1,128)} %param.17) | copy-start | bytes 628
  137.1 248.5 %all-gather.2.cloned.1.call-start = ((), (), s32[]{:S(2)}) async-start(), calls=%async_computation.2 | async-start | bytes 8912896 | tf_op jit(solution)/shard_map/all_gather | solution.py:72
Sparse Core Ops, SparseCore 0:
  137.2 150.3 reduce-scatter.1
  314.4 71.2 all-gather.1
where the time goes:
time: 425 us; the launch traced here: 424 us
  waiting for transfers between devices  261 us (61%)
  local copies, waits for them, and re-layouts  63 us (15%)
  matrix products  43 us (10%)
  other arithmetic  30.5 us (7%)
  between operations  16.6 us (4%)
  loops' own time  8.52 us (2%)
    reduce_scatter x1, waiting for transfers between devices, on_device(): mine = lax.psum_scatter(outgoing, 'dp', scatter_dimension=0, tiled=True)  149 us
    all_gather x1, waiting for transfers between devices, on_device(): every_inverse = lax.all_gather(inverse, 'dp', axis=0, tiled=True)  62.3 us
    ppermute x1, waiting for transfers between devices, passed_along(): return lax.ppermute(block, axis, route)  50.3 us
    unnamed x5, local copies, waits for them, and re-layouts  20.1 us
    dot_general x1, matrix products, on_device(): jnp.einsum('tkb,tkc->kbc', shaped_a, shaped_a, preferred_element_type=jnp...  18.6 us
    gather x1, local copies, waits for them, and re-layouts, on_device(): jnp.take(jnp.concatenate([partial_value, zero_block], axis=0), block_of,...  13.7 us
    select_n x2, other arithmetic, on_device(): jnp.take(jnp.concatenate([partial_value, zero_block], axis=0), block_of,...  11.6 us
    reshape x1, local copies, waits for them, and re-layouts, on_device(): half = half.reshape(model_blocks, BLOCK, column_count)  9.95 us
  transfers between devices with their start and end apart: 3, of which 3 were waited for; matrix products, arithmetic and copies ran while one was open for 11% of the time, Pallas kernels for 0%

commit v1 on v0

v1 whole, which is shorter than its diff:
```python
import functools

import jax
import jax.numpy as jnp
from jax import lax
from jax.experimental import pallas as pl
from jax.experimental.pallas import tpu as pltpu
from jax.sharding import PartitionSpec as P

BLOCK = 256
HALF = 128
ROWS = 272
DAMPING = 0.05
F32 = jnp.float32
BF16 = jnp.bfloat16
MESH = pl.DeviceIdType.MESH


def iotas(rows, columns):
    return (
        lax.broadcasted_iota(jnp.int32, (rows, columns), 0),
        lax.broadcasted_iota(jnp.int32, (rows, columns), 1),
    )


def store_diagonals(dst, i, both):
    high = both.astype(BF16)
    low = both - high.astype(F32)
    dst[i, pl.ds(BLOCK, 16), :] = jnp.concatenate([high.astype(F32), low], axis=0).astype(BF16)


def store_packed(dst, i, full):
    row, column = iotas(HALF, HALF)
    first, off, last = full[:HALF, :HALF], full[:HALF, HALF:], full[HALF:, HALF:]
    dst[i, pl.ds(0, HALF), :] = jnp.where(row <= column, first, last).astype(BF16)
    dst[i, pl.ds(HALF, HALF), :] = off.astype(BF16)
    d_first = jnp.sum(jnp.where(row == column, first, 0.0), axis=0, keepdims=True)
    d_last = jnp.sum(jnp.where(row == column, last, 0.0), axis=0, keepdims=True)
    row8, _ = iotas(8, HALF)
    both = jnp.where(row8 == 0, d_first, jnp.where(row8 == 1, d_last, 0.0))
    store_diagonals(dst, i, both)


def add_packed(dst, di, a, ai, b, bi):
    dst[di, pl.ds(0, BLOCK), :] = (
        a[ai, pl.ds(0, BLOCK), :].astype(F32) + b[bi, pl.ds(0, BLOCK), :].astype(F32)
    ).astype(BF16)
    total = a[ai, pl.ds(BLOCK, 16), :].astype(F32) + b[bi, pl.ds(BLOCK, 16), :].astype(F32)
    store_diagonals(dst, di, total[:8] + total[8:])


def unpack(selected, off, both):
    row, column = iotas(HALF, HALF)
    flipped = selected.T
    first = jnp.where(row == column, both[0:1], jnp.where(row <= column, selected, flipped))
    last = jnp.where(row == column, both[1:2], jnp.where(row > column, selected, flipped))
    return jnp.concatenate(
        [jnp.concatenate([first, off], axis=1), jnp.concatenate([off.T, last], axis=1)], axis=0
    )


def load_full(src, i):
    tail = src[i, pl.ds(BLOCK, 16), :].astype(F32)
    return unpack(
        src[i, pl.ds(0, HALF), :].astype(F32),
        src[i, pl.ds(HALF, HALF), :].astype(F32),
        tail[:8] + tail[8:],
    )


def load_full_sum(a, ai, b, bi):
    both = [
        a[ai, pl.ds(start, size), :].astype(F32) + b[bi, pl.ds(start, size), :].astype(F32)
        for start, size in ((0, HALF), (HALF, HALF), (BLOCK, 16))
    ]
    return unpack(both[0], both[1], both[2][:8] + both[2][8:])


def split(x):
    high = x.astype(BF16)
    return high, (x - high.astype(F32)).astype(BF16)


def product(a, b):
    a_high, a_low = split(a)
    b_high, b_low = split(b)
    left = jnp.concatenate([a_high, a_high, a_low], axis=1)
    right = jnp.concatenate([b_high, b_low, b_high], axis=0)
    return jnp.dot(left, right, preferred_element_type=F32)


def newton(matrix, count):
    row, column = iotas(BLOCK, BLOCK)
    eye = jnp.where(row == column, 1.0, 0.0).astype(F32)
    norm = jnp.max(jnp.sum(jnp.abs(matrix), axis=0, keepdims=True), axis=1, keepdims=True)
    scale = 1.0 / norm
    residual = eye - scale * matrix
    approx = scale * (eye + residual)
    chosen = approx
    residual = product(residual, residual)
    for turn in range(1, 4):
        if turn < 3:
            both = product(jnp.concatenate([residual, approx], axis=0), residual)
            approx = approx + both[BLOCK:]
            residual = both[:BLOCK]
        else:
            approx = approx + product(approx, residual)
        chosen = jnp.where(count > turn, approx, chosen)
    return chosen


def exchange_kernel(
    tokens, sweeps, acts, grads, head, inv_a, inv_g,
    x_a, x_g, gs1, go1, gr1, gs2, go2, gr2, gs3, go3, gr3, gs4, gx0, gx1, x3, r2, y3, y2, dx3, dr2, dy3, dy2,
    as1, ao1, ar1, as2, ao2, ar2, as3, ao3, ar3, as4, ao4, ar4, load_sem, send_sem, recv_sem,
):
    section = lax.axis_index("section")
    dp = lax.axis_index("dp")
    core = lax.rem(dp, 2)
    y = lax.rem(dp // 2, 4)
    x = dp // 8
    y_low, y_high = lax.rem(y, 2), y // 2
    y_odd = lax.rem(y_low + y_high, 2)
    near = y + 1 - 2 * y_low
    far = 3 - y
    first_y = jnp.where(core == 0, near, far)
    second_y = jnp.where(core == 0, far, near)
    b1 = jnp.where(core == 0, y_odd, y_high)
    b2 = jnp.where(core == 0, y_high, y_odd)
    n1, n2 = 1 - b1, 1 - b2
    p_core = (section, dp + 1 - 2 * core)
    p_y1 = (section, x * 8 + first_y * 2 + core)
    p_y2 = (section, x * 8 + second_y * 2 + core)
    p_x = (section, lax.rem(dp + 8, 16))
    below, above = lax.rem(section + 7, 8), lax.rem(section + 1, 8)
    p_straight = (below, dp)
    p_cross = (below, lax.rem(dp + 8, 16))

    def rdma(i, src, dst, target):
        return pltpu.make_async_remote_copy(
            src_ref=src, dst_ref=dst, send_sem=send_sem.at[i], recv_sem=recv_sem.at[i],
            device_id=target, device_id_type=MESH,
        )

    g_chunk, a_chunk = x_g.shape[1] // 2, x_a.shape[1] // 4

    def load_g(i, src):
        part = pl.ds(pl.multiple_of(i * g_chunk, BLOCK), g_chunk)
        return pltpu.make_async_copy(src.at[:, part], x_g.at[:, part], load_sem.at[i])

    def load_a(i):
        part = pl.ds(i * a_chunk, a_chunk)
        return pltpu.make_async_copy(acts.at[0, :, part], x_a.at[:, part], load_sem.at[2 + i])

    g_order = (1 - core, core)

    @pl.when(section == 0)
    def _():
        for i in range(2):
            pltpu.make_async_copy(
                head.at[:, pl.ds(i * g_chunk, g_chunk)], x_g.at[:, pl.ds(i * g_chunk, g_chunk)], load_sem.at[i]
            ).start()

    @pl.when(section > 0)
    def _():
        for i in range(2):
            pltpu.make_async_copy(
                grads.at[0, :, pl.ds(i * g_chunk, g_chunk)], x_g.at[:, pl.ds(i * g_chunk, g_chunk)], load_sem.at[i]
            ).start()

    for i in range(4):
        load_a(i).start()

    barrier = pltpu.get_barrier_semaphore()
    greeted = (p_core, p_y1, p_y2, p_x, p_straight, p_cross, (above, dp), (above, lax.rem(dp + 8, 16)))
    for target in greeted:
        pl.semaphore_signal(barrier, inc=1, device_id=target, device_id_type=MESH)

    def outer(ref, block):
        columns = pl.ds(pl.multiple_of(block * BLOCK, BLOCK), BLOCK)
        tile = ref[:, columns]
        return lax.dot_general(tile, tile, (((0,), (0,)), ((), ())), preferred_element_type=F32)

    def g_partials(dst, which):
        @pl.loop(0, 10)
        def _(i):
            store_packed(dst, i, outer(x_g, which * 10 + i))

    def a_block(q, j):
        q_core = q // 8
        h1, h2, h3 = lax.rem(q // 4, 2), lax.rem(q // 2, 2), lax.rem(q, 2)
        odd = lax.rem(h1 + h2, 2)
        high = jnp.where(q_core == 0, h2, h1)
        low = odd
        owner = h3 * 8 + (high * 2 + low) * 2 + q_core
        return owner * 2 + j

    def a_partials(dst, which, start, stop):
        @pl.loop(start, stop)
        def _(i):
            store_packed(dst, i, outer(x_a, a_block(which * 8 + i // 2, lax.rem(i, 2))))

    def add_blocks(dst, size, a, b, start):
        @pl.loop(0, size)
        def _(i):
            add_packed(dst, i, a, start + i, b, start + i)

    load_g(0, head).wait()
    load_g(1, head).wait()
    g_partials(gs1, 1 - core)
    pl.semaphore_wait(barrier, len(greeted))
    g_core = rdma(0, gs1, gr1, p_core)
    g_core.start()
    g_partials(go1, core)
    g_core.wait()
    add_blocks(gs2, 5, go1, gr1, n1 * 5)
    g_y1 = rdma(1, gs2, gr2, p_y1)
    g_y1.start()
    add_blocks(go2, 5, go1, gr1, b1 * 5)
    for i in range(4):
        load_a(i).wait()
    a_partials(as1, 1 - core, 0, 16)
    a_core = rdma(9, as1, ar1, p_core)
    a_core.start()
    a_partials(ao1, core, 0, 4)
    g_y1.wait()
    add_blocks(gs3, 3, go2, gr2, n2 * 2)
    g_y2 = rdma(2, gs3, gr3, p_y2)
    g_y2.start()
    add_blocks(go3, 3, go2, gr2, b2 * 2)
    a_partials(ao1, core, 4, 16)
    g_y2.wait()
    g_over = []
    for i in range(3):
        add_packed(gs4, i, go3, i, gr3, i)
        for base, dst, target in ((3, gx0, p_straight), (6, gx1, p_cross)):
            copy = rdma(base + i, gs4.at[i], dst.at[i], target)
            copy.start()
            g_over.append(copy)
    a_core.wait()
    add_blocks(as2, 8, ao1, ar1, n1 * 8)
    a_y1 = rdma(10, as2, ar2, p_y1)
    a_y1.start()
    add_blocks(ao2, 8, ao1, ar1, b1 * 8)
    a_y1.wait()
    add_blocks(as3, 4, ao2, ar2, n2 * 4)
    a_y2 = rdma(11, as3, ar3, p_y2)
    a_y2.start()
    add_blocks(ao3, 4, ao2, ar2, b2 * 4)

    row, column = iotas(BLOCK, BLOCK)
    damp = jnp.where(row == column, DAMPING, 0.0).astype(F32)
    hidden_blocks = x_a.shape[1] // BLOCK
    g_first = core * 10 + b1 * 5 + b2 * 2
    for i in range(3):
        g_over[2 * i].wait()
        g_over[2 * i + 1].wait()
        factor = load_full_sum(gx0, i, gx1, i) * (1.0 / tokens) + damp
        inverse = newton(factor, sweeps[0, hidden_blocks + g_first + i])
        store_packed(x3, i, inverse)
    x3_y1 = rdma(14, x3, y3, p_y1)
    x3_y2 = rdma(13, x3.at[pl.ds(b2, 2)], r2, p_y2)
    x3_core = rdma(16, x3, dx3, p_core)
    x3_y2.start()
    x3_y1.start()
    x3_core.start()

    def expand(src, size, start):
        @pl.loop(0, size)
        def _(i):
            inv_g[start + i, :, :] = load_full(src, i).astype(BF16)

    a_y2.wait()
    add_blocks(as4, 2, ao3, ar3, (1 - x) * 2)
    a_x = rdma(12, as4, ar4, p_x)
    a_x.start()
    add_blocks(ao4, 2, ao3, ar3, x * 2)
    expand(x3, 3, g_first)
    x3_y2.wait()
    r2_y1 = rdma(15, r2, y2, p_y1)
    r2_core = rdma(17, r2, dr2, p_core)
    r2_y1.start()
    r2_core.start()
    expand(r2, 2, core * 10 + b1 * 5 + n2 * 3)
    x3_y1.wait()
    y3_core = rdma(18, y3, dy3, p_core)
    y3_core.start()
    expand(y3, 3, core * 10 + n1 * 5 + b2 * 2)
    r2_y1.wait()
    y2_core = rdma(19, y2, dy2, p_core)
    y2_core.start()
    expand(y2, 2, core * 10 + n1 * 5 + n2 * 3)
    other = (1 - core) * 10
    x3_core.wait()
    expand(dx3, 3, other + b2 * 5 + b1 * 2)
    r2_core.wait()
    expand(dr2, 2, other + b2 * 5 + n1 * 3)
    a_x.wait()
    for j in range(2):
        factor = load_full_sum(ao4, j, ar4, j) * (1.0 / tokens) + damp
        inv_a[j, :, :] = newton(factor, sweeps[0, dp * 2 + j]).astype(BF16)
    y3_core.wait()
    expand(dy3, 3, other + n2 * 5 + b1 * 2)
    y2_core.wait()
    expand(dy2, 2, other + n2 * 5 + n1 * 3)


def packed(count):
    return pltpu.VMEM((count, ROWS, HALF), BF16)


def exchange(tokens, sweeps, acts, grads, head):
    hbm = pl.BlockSpec(memory_space=pl.ANY)
    vmem = pl.BlockSpec(memory_space=pltpu.VMEM)
    rows = acts.shape[1]
    model_blocks = grads.shape[2] // BLOCK
    counts = (10, 10, 10, 5, 5, 5, 3, 3, 3, 3, 3, 3, 3, 2, 3, 2, 3, 2, 3, 2)
    a_counts = (16, 16, 16, 8, 8, 8, 4, 4, 4, 2, 2, 2)
    return pl.pallas_call(
        functools.partial(exchange_kernel, tokens),
        out_shape=(
            jax.ShapeDtypeStruct((2, BLOCK, BLOCK), BF16),
            jax.ShapeDtypeStruct((model_blocks, BLOCK, BLOCK), BF16),
        ),
        in_specs=[pl.BlockSpec(memory_space=pltpu.SMEM), hbm, hbm, hbm],
        out_specs=(vmem, vmem),
        scratch_shapes=[
            pltpu.VMEM((rows, acts.shape[2]), BF16),
            pltpu.VMEM((rows, grads.shape[2]), BF16),
            *[packed(n) for n in counts],
            *[packed(n) for n in a_counts],
            pltpu.SemaphoreType.DMA((6,)),
            pltpu.SemaphoreType.DMA((20,)),
            pltpu.SemaphoreType.DMA((20,)),
        ],
        compiler_params=pltpu.CompilerParams(
            collective_id=0, has_side_effects=True, vmem_limit_bytes=60 * 1024 * 1024
        ),
        name="exchange",
    )(sweeps, acts, grads, head)


def apply_kernel(weights, inv_a, inv_g, out):
    halves = [
        jnp.dot(weights[0, :, j * BLOCK : (j + 1) * BLOCK], inv_a[j], preferred_element_type=F32).astype(BF16)
        for j in range(2)
    ]
    half = jnp.concatenate(halves, axis=1)
    out[0, :, :] = jnp.dot(inv_g[0], half, preferred_element_type=F32).astype(BF16)


def apply(weights, inv_a, inv_g):
    _, rows, columns = weights.shape
    return pl.pallas_call(
        apply_kernel,
        out_shape=jax.ShapeDtypeStruct(weights.shape, BF16),
        grid=(rows // BLOCK,),
        in_specs=[
            pl.BlockSpec((1, BLOCK, columns), lambda k: (0, k, 0)),
            pl.BlockSpec((2, BLOCK, BLOCK), lambda k: (0, 0, 0)),
            pl.BlockSpec((1, BLOCK, BLOCK), lambda k: (k, 0, 0)),
        ],
        out_specs=pl.BlockSpec((1, BLOCK, columns), lambda k: (0, k, 0)),
        name="apply",
    )(weights, inv_a, inv_g)


def on_device(acts, input_grads, head_grads, weight_grad, sweeps):
    tokens = acts.shape[1] * lax.axis_size("dp")
    inv_a, inv_g = exchange(tokens, sweeps, acts, input_grads, head_grads)
    return apply(weight_grad, inv_a, inv_g)


def solution(mesh):
    return jax.shard_map(
        on_device,
        mesh=mesh,
        in_specs=(
            P("section", "dp", None),
            P("section", "dp", None),
            P("dp", None),
            P("section", None, "dp"),
            P("section", None),
        ),
        out_specs=P("section", None, "dp"),
        check_vma=False,
    )
```

time: 425 us -> 69.4 us (0.16)
  the two profiles are of different devices: /device:TPU:1 before, /device:TPU:0 now
where the time goes in v1:
time: 69.4 us; the launch traced here: 68.9 us
  Pallas kernels  68.9 us (99%)
    pallas_call x1, Pallas kernels, exchange(): pl.pallas_call(functools.partial(exchange_kernel, tokens), out_shape=(jax...  52.2 us
    pallas_call x1, Pallas kernels, apply(): pl.pallas_call(apply_kernel, out_shape=jax.ShapeDtypeStruct(weights.shape...  16.7 us

profile of v1, /device:TPU:0, one launch (start us, length us, event | category | flops | bytes accessed | tf_op | source)
XLA Modules:
  0.0 68.9 jit_solution(5627196153844871396)
XLA Ops:
  0.0 52.2 %exchange.1 = (bf16[2,256,256]{2,1,0:T(8,128)(2,1)}, bf16[20,256,256]{2,1,0:T(8,128)(2,1)}) custom-call(s32[1,52]{1,0:T(1,128)} %sweeps.1, bf16[1,384,8192]{2,1,0:T(8,128)(2,1)} %acts.1, bf16[1,384,5120]{2,1,0:T(8,128)(2,1)} %grads.1, bf16[384,5120]{1,0:T(8,128)(2,1)} %head.1), custom_call_target="tpu_custom_call" | custom-call | tf_op jit(solution)/shard_map/exchange/pallas_call | solution.py:319
  52.2 16.7 %apply.1 = bf16[1,5120,512]{2,1,0:T(8,128)(2,1)} custom-call(bf16[1,5120,512]{2,1,0:T(8,128)(2,1)} %weights.1, bf16[2,256,256]{2,1,0:T(8,128)(2,1)} %get-tuple-element.7.inv_a, bf16[20,256,256]{2,1,0:T(8,128)(2,1)} %get-tuple-element.8.inv_g), custom_call_target="tpu_custom_call" | custom-call | tf_op jit(solution)/shard_map/apply/pallas_call | solution.py:354

commit v2 on v1

v2 whole, which is shorter than its diff:
```python
import functools

import jax
import jax.numpy as jnp
from jax import lax
from jax.experimental import pallas as pl
from jax.experimental.pallas import tpu as pltpu
from jax.sharding import PartitionSpec as P

BLOCK = 256
HALF = 128
ROWS = 272
DAMPING = 0.05
F32 = jnp.float32
BF16 = jnp.bfloat16
MESH = pl.DeviceIdType.MESH


def iotas(rows, columns):
    return (
        lax.broadcasted_iota(jnp.int32, (rows, columns), 0),
        lax.broadcasted_iota(jnp.int32, (rows, columns), 1),
    )


def store_diagonals(dst, i, both):
    high = both.astype(BF16)
    low = both - high.astype(F32)
    dst[i, pl.ds(BLOCK, 16), :] = jnp.concatenate([high.astype(F32), low], axis=0).astype(BF16)


def store_packed(dst, i, full):
    row, column = iotas(HALF, HALF)
    first, off, last = full[:HALF, :HALF], full[:HALF, HALF:], full[HALF:, HALF:]
    dst[i, pl.ds(0, HALF), :] = jnp.where(row <= column, first, last).astype(BF16)
    dst[i, pl.ds(HALF, HALF), :] = off.astype(BF16)
    d_first = jnp.sum(jnp.where(row == column, first, 0.0), axis=0, keepdims=True)
    d_last = jnp.sum(jnp.where(row == column, last, 0.0), axis=0, keepdims=True)
    row8, _ = iotas(8, HALF)
    both = jnp.where(row8 == 0, d_first, jnp.where(row8 == 1, d_last, 0.0))
    store_diagonals(dst, i, both)


def add_packed(dst, di, a, ai, b, bi):
    dst[di, pl.ds(0, BLOCK), :] = (
        a[ai, pl.ds(0, BLOCK), :].astype(F32) + b[bi, pl.ds(0, BLOCK), :].astype(F32)
    ).astype(BF16)
    total = a[ai, pl.ds(BLOCK, 16), :].astype(F32) + b[bi, pl.ds(BLOCK, 16), :].astype(F32)
    store_diagonals(dst, di, total[:8] + total[8:])


def unpack(selected, off, both):
    row, column = iotas(HALF, HALF)
    flipped = selected.T
    first = jnp.where(row == column, both[0:1], jnp.where(row <= column, selected, flipped))
    last = jnp.where(row == column, both[1:2], jnp.where(row > column, selected, flipped))
    return jnp.concatenate(
        [jnp.concatenate([first, off], axis=1), jnp.concatenate([off.T, last], axis=1)], axis=0
    )


def load_full(src, i):
    tail = src[i, pl.ds(BLOCK, 16), :].astype(F32)
    return unpack(
        src[i, pl.ds(0, HALF), :].astype(F32),
        src[i, pl.ds(HALF, HALF), :].astype(F32),
        tail[:8] + tail[8:],
    )


def load_full_sum(a, ai, b, bi):
    both = [
        a[ai, pl.ds(start, size), :].astype(F32) + b[bi, pl.ds(start, size), :].astype(F32)
        for start, size in ((0, HALF), (HALF, HALF), (BLOCK, 16))
    ]
    return unpack(both[0], both[1], both[2][:8] + both[2][8:])


def split(x):
    high = x.astype(BF16)
    return high, (x - high.astype(F32)).astype(BF16)


def product(a, b):
    a_high, a_low = split(a)
    b_high, b_low = split(b)
    left = jnp.concatenate([a_high, a_high, a_low], axis=1)
    right = jnp.concatenate([b_high, b_low, b_high], axis=0)
    return jnp.dot(left, right, preferred_element_type=F32)


def newton(matrices, counts):
    row, column = iotas(BLOCK, BLOCK)
    eye = jnp.where(row == column, 1.0, 0.0).astype(F32)
    state = []
    for matrix in matrices:
        norm = jnp.max(jnp.sum(jnp.abs(matrix), axis=0, keepdims=True), axis=1, keepdims=True)
        scale = 1.0 / norm
        residual = eye - scale * matrix
        approx = scale * (eye + residual)
        state.append((approx, residual))
    chosen = [approx for approx, _ in state]
    state = [(approx, product(residual, residual)) for approx, residual in state]
    for turn in range(1, 4):
        if turn < 3:
            both = [product(jnp.concatenate([residual, approx], axis=0), residual) for approx, residual in state]
            state = [(approx + b[BLOCK:], b[:BLOCK]) for (approx, _), b in zip(state, both)]
        else:
            state = [(approx + product(approx, residual), None) for approx, residual in state]
        chosen = [jnp.where(count > turn, now, old) for count, (now, _), old in zip(counts, state, chosen)]
    return chosen


def exchange_kernel(
    tokens, sweeps_hbm, acts, grads, head, weights, out, sweeps,
    x_a, x_g, w, half, gs1, go1, gr1, gs2, gr2, gs3, gr3, gs4, gx0, gx1,
    own, r2, y3, y2, d_own, d_r2, d_y3, d_y2,
    as1, ao1, ar1, as2, ar2, as3, ar3, as4, ar4, inv_a, load_sem, send_sem, recv_sem,
):
    section = lax.axis_index("section")
    dp = lax.axis_index("dp")
    core = lax.rem(dp, 2)
    y = lax.rem(dp // 2, 4)
    x = dp // 8
    y_low, y_high = lax.rem(y, 2), y // 2
    y_odd = lax.rem(y_low + y_high, 2)
    near = y + 1 - 2 * y_low
    far = 3 - y
    first_y = jnp.where(core == 0, near, far)
    second_y = jnp.where(core == 0, far, near)
    b1 = jnp.where(core == 0, y_odd, y_high)
    b2 = jnp.where(core == 0, y_high, y_odd)
    n1, n2 = 1 - b1, 1 - b2
    crossed = lax.rem(dp + 8, 16)
    below, above = lax.rem(section + 7, 8), lax.rem(section + 1, 8)
    p_core = (section, dp + 1 - 2 * core)
    p_y1 = (section, x * 8 + first_y * 2 + core)
    p_y2 = (section, x * 8 + second_y * 2 + core)
    p_x = (section, crossed)
    p_straight = (below, dp)
    p_cross = (below, crossed)
    used = []

    def send(src, dst, target):
        i = len(used)
        used.append(i)
        copy = pltpu.make_async_remote_copy(
            src_ref=src, dst_ref=dst, send_sem=send_sem.at[i], recv_sem=recv_sem.at[i],
            device_id=target, device_id_type=MESH,
        )
        copy.start()
        return copy

    g_chunk, a_chunk, w_chunk = x_g.shape[1] // 2, x_a.shape[1] // 2, w.shape[0] // 2
    model_blocks, hidden_blocks = x_g.shape[1] // BLOCK, x_a.shape[1] // BLOCK

    def load_g(i, src):
        part = pl.ds(i * g_chunk, g_chunk)
        return pltpu.make_async_copy(src.at[:, part], x_g.at[:, part], load_sem.at[i])

    def load_a(i):
        part = pl.ds(i * a_chunk, a_chunk)
        return pltpu.make_async_copy(acts.at[0, :, part], x_a.at[:, part], load_sem.at[2 + i])

    def load_w(i):
        part = pl.ds(i * w_chunk, w_chunk)
        return pltpu.make_async_copy(weights.at[0, part, :], w.at[part, :], load_sem.at[4 + i])

    @pl.when(section == 0)
    def _():
        for i in range(2):
            load_g(i, head).start()

    @pl.when(section > 0)
    def _():
        for i in range(2):
            load_g(i, grads.at[0]).start()

    load_sweeps = pltpu.make_async_copy(sweeps_hbm, sweeps, load_sem.at[6])
    load_sweeps.start()
    barrier = pltpu.get_barrier_semaphore()
    greeted = (p_core, p_y1, p_y2, p_x, p_straight, p_cross, (above, dp), (above, crossed))
    for target in greeted:
        pl.semaphore_signal(barrier, inc=1, device_id=target, device_id_type=MESH)

    def outer(ref, block):
        columns = pl.ds(pl.multiple_of(block * BLOCK, BLOCK), BLOCK)
        tile = ref[:, columns]
        return lax.dot_general(tile, tile, (((0,), (0,)), ((), ())), preferred_element_type=F32)

    def place(k, bit):
        return (1 - bit) * 3 + k if k < 2 else 2 if k == 2 else bit * 3 + k - 3

    def g_partials(dst, at, group, bit):
        for k in range(5):
            store_packed(dst, at + k, outer(x_g, group * 5 + place(k, bit)))

    def a_partials(dst, at, of_core, first, second):
        @pl.loop(0, 2)
        def _(e):
            bit = jnp.where(e == 0, 1 - second, second)
            for u in range(2):
                owner = (1 - x if u == 0 else x) * 8
                for j in range(2):
                    for_core_0 = owner + (bit * 2 + lax.rem(first + bit, 2)) * 2
                    for_core_1 = owner + (first * 2 + lax.rem(first + bit, 2)) * 2 + 1
                    block = jnp.where(of_core == 0, for_core_0, for_core_1) * 2 + j
                    store_packed(dst, at + 4 * e + 2 * u + j, outer(x_a, block))

    def add_blocks(dst, di, size, a, ai, b, bi):
        @pl.loop(0, size)
        def _(i):
            add_packed(dst, di + i, a, ai + i, b, bi + i)

    load_g(0, head).wait()
    load_g(1, head).wait()
    for i in range(2):
        load_a(i).start()
    o_core = 1 - core
    g_partials(gs1, 0, o_core * 2 + n2, b1)
    pl.semaphore_wait(barrier, len(greeted))
    g_core = [send(gs1.at[pl.ds(0, 5)], gr1.at[pl.ds(0, 5)], p_core)]
    g_partials(go1, 0, core * 2 + n1, b2)
    g_core[0].wait()
    g_y1 = []
    for k in range(5):
        add_packed(gs2, k, go1, k, gr1, k)
        g_y1.append(send(gs2.at[k], gr2.at[k], p_y1))
    g_partials(gs1, 5, o_core * 2 + b2, b1)
    g_core.append(send(gs1.at[pl.ds(5, 5)], gr1.at[pl.ds(5, 5)], p_core))
    g_partials(go1, 5, core * 2 + b1, b2)
    for i in range(2):
        load_a(i).wait()
    for i in range(2):
        load_w(i).start()
    a_partials(as1, 0, o_core, n2, b1)
    a_core = [send(as1.at[pl.ds(0, 8)], ar1.at[pl.ds(0, 8)], p_core)]
    a_partials(ao1, 0, core, n1, b2)
    g_core[1].wait()
    add_blocks(go1, 5, 5, go1, 5, gr1, 5)
    g_y2 = []
    for k in range(3):
        g_y1[k].wait()
        add_packed(gs3, k, go1, 5 + k, gr2, k)
        g_y2.append(send(gs3.at[k], gr3.at[k], p_y2))
    a_core[0].wait()
    a_y1 = []
    for i in range(2):
        add_blocks(as2, 4 * i, 4, ao1, 4 * i, ar1, 4 * i)
        a_y1.append(send(as2.at[pl.ds(4 * i, 4)], ar2.at[pl.ds(4 * i, 4)], p_y1))
    a_partials(as1, 8, o_core, b2, b1)
    a_core.append(send(as1.at[pl.ds(8, 8)], ar1.at[pl.ds(8, 8)], p_core))
    g_over = []
    for k in range(3):
        mine = (8, 9, 7)[k]
        g_y2[k].wait()
        if k < 2:
            g_y1[3 + k].wait()
        add_packed(go1, mine, go1, mine, gr2, mine - 5)
        add_packed(gs4, k, go1, mine, gr3, k)
        g_over.append((send(gs4.at[k], gx0.at[k], p_straight), send(gs4.at[k], gx1.at[k], p_cross)))
    a_partials(ao1, 8, core, b1, b2)
    a_core[1].wait()
    add_blocks(ao1, 8, 8, ao1, 8, ar1, 8)
    a_y1[0].wait()
    add_blocks(as3, 0, 4, ao1, 8, ar2, 0)
    a_y2 = [send(as3.at[pl.ds(2 * i, 2)], ar3.at[pl.ds(2 * i, 2)], p_y2) for i in range(2)]
    a_y1[1].wait()
    add_blocks(ao1, 12, 4, ao1, 12, ar2, 4)
    load_sweeps.wait()
    row, column = iotas(BLOCK, BLOCK)
    damp = jnp.where(row == column, DAMPING, 0.0).astype(F32)
    mean = 1.0 / tokens
    here, there = core * 10, o_core * 10
    g_own, g_r2, g_own_core, g_y3_core = [], [], [], []

    def g_invert(k):
        g_over[k][0].wait()
        g_over[k][1].wait()
        factor = load_full_sum(gx0, k, gx1, k) * mean + damp
        at = here + b1 * 5 + (b2 * 3 + k if k < 2 else 2)
        store_packed(own, k, newton([factor], [sweeps[0, hidden_blocks + at]])[0])
        if k < 2:
            g_r2.append(send(own.at[k], r2.at[k], p_y2))
        g_own.append(send(own.at[k], y3.at[k], p_y1))
        g_own_core.append(send(own.at[k], d_own.at[k], p_core))

    g_invert(0)
    a_y2[0].wait()
    add_blocks(as4, 0, 2, ao1, 12, ar3, 0)
    a_x = send(as4, ar4, p_x)
    a_y2[1].wait()
    add_blocks(ao1, 14, 2, ao1, 14, ar3, 2)
    g_invert(1)
    g_invert(2)
    for i in range(2):
        load_w(i).wait()
    relayed, y2_core = [], []

    def relay(k):
        g_r2[k].wait()
        relayed.append((send(r2.at[k], y2.at[k], p_y1), send(r2.at[k], d_r2.at[k], p_core)))

    def pass_own(k):
        g_own[k].wait()
        g_y3_core.append(send(y3.at[k], d_y3.at[k], p_core))

    def pass_y2(k):
        relayed[k][0].wait()
        y2_core.append(send(y2.at[k], d_y2.at[k], p_core))

    relay(0)
    relay(1)
    a_x.wait()
    factors = [load_full_sum(ao1, 14 + j, ar4, j) * mean + damp for j in range(2)]
    for j, inverse in enumerate(newton(factors, [sweeps[0, dp * 2 + j] for j in range(2)])):
        inv_a[j, :, :] = inverse.astype(BF16)
    for k in range(3):
        pass_own(k)

    def halves(start, stop):
        @pl.loop(start // 2, stop // 2)
        def _(k):
            rows = pl.ds(pl.multiple_of(k * 2 * BLOCK, 2 * BLOCK), 2 * BLOCK)
            for j in range(2):
                columns = slice(j * BLOCK, (j + 1) * BLOCK)
                half[rows, columns] = jnp.dot(w[rows, columns], inv_a[j], preferred_element_type=F32).astype(BF16)

    halves(0, 10)
    pass_y2(0)
    pass_y2(1)
    halves(10, model_blocks)

    def apply(src, i, block):
        rows = pl.ds(pl.multiple_of(block * BLOCK, BLOCK), BLOCK)
        inverse = load_full(src, i).astype(BF16)
        out[0, rows, :] = jnp.dot(inverse, half[rows, :], preferred_element_type=F32).astype(BF16)

    def apply_own(src, group, bit):
        for k in range(3):
            apply(src, k, group + (bit * 3 + k if k < 2 else 2))

    def apply_r2(src, group, bit):
        for k in range(2):
            apply(src, k, group + bit * 3 + k)

    apply_own(own, here + b1 * 5, b2)
    apply_r2(r2, here + b1 * 5, n2)
    apply_own(y3, here + n1 * 5, b2)
    apply_r2(y2, here + n1 * 5, n2)
    for k in range(3):
        g_own_core[k].wait()
    apply_own(d_own, there + b2 * 5, b1)
    for k in range(2):
        relayed[k][1].wait()
    apply_r2(d_r2, there + b2 * 5, n1)
    for k in range(3):
        g_y3_core[k].wait()
    apply_own(d_y3, there + n2 * 5, b1)
    for k in range(2):
        y2_core[k].wait()
    apply_r2(d_y2, there + n2 * 5, n1)


def packed(count):
    return pltpu.VMEM((count, ROWS, HALF), BF16)


def exchange(tokens, sweeps, acts, grads, head, weights):
    hbm = pl.BlockSpec(memory_space=pltpu.HBM)
    vmem = pl.BlockSpec(memory_space=pltpu.VMEM)
    operands = [pltpu.with_memory_space_constraint(a, pltpu.HBM) for a in (sweeps, acts, grads, head, weights)]
    rows = acts.shape[1]
    g_counts = (10, 10, 10, 5, 5, 3, 3, 3, 3, 3)
    gather_counts = (3, 2, 3, 2, 3, 2, 3, 2)
    a_counts = (16, 16, 16, 8, 8, 4, 4, 2, 2)
    return pl.pallas_call(
        functools.partial(exchange_kernel, tokens),
        out_shape=pltpu.VMEM(weights.shape, BF16),
        in_specs=[hbm] * 5,
        out_specs=vmem,
        scratch_shapes=[
            pltpu.SMEM(sweeps.shape, jnp.int32),
            pltpu.VMEM((rows, acts.shape[2]), BF16),
            pltpu.VMEM((rows, grads.shape[2]), BF16),
            pltpu.VMEM(weights.shape[1:], BF16),
            pltpu.VMEM(weights.shape[1:], BF16),
            *[packed(n) for n in g_counts + gather_counts + a_counts],
            pltpu.VMEM((2, BLOCK, BLOCK), BF16),
            pltpu.SemaphoreType.DMA((7,)),
            pltpu.SemaphoreType.DMA((41,)),
            pltpu.SemaphoreType.DMA((41,)),
        ],
        compiler_params=pltpu.CompilerParams(
            collective_id=0, has_side_effects=True, vmem_limit_bytes=44 * 1024 * 1024
        ),
        name="exchange",
    )(*operands)


def store_kernel(src, dst, sem):
    copy = pltpu.make_async_copy(src, dst, sem)
    copy.start()
    copy.wait()


def store(update):
    return pl.pallas_call(
        store_kernel,
        out_shape=jax.ShapeDtypeStruct(update.shape, update.dtype),
        in_specs=[pl.BlockSpec(memory_space=pltpu.VMEM)],
        out_specs=pl.BlockSpec(memory_space=pltpu.HBM),
        scratch_shapes=[pltpu.SemaphoreType.DMA],
        compiler_params=pltpu.CompilerParams(vmem_limit_bytes=1024 * 1024),
        name="store",
    )(update)


def on_device(acts, input_grads, head_grads, weight_grad, sweeps):
    tokens = acts.shape[1] * lax.axis_size("dp")
    return store(exchange(tokens, sweeps, acts, input_grads, head_grads, weight_grad))


def solution(mesh):
    return jax.shard_map(
        on_device,
        mesh=mesh,
        in_specs=(
            P("section", "dp", None),
            P("section", "dp", None),
            P("dp", None),
            P("section", None, "dp"),
            P("section", None),
        ),
        out_specs=P("section", None, "dp"),
        check_vma=False,
    )
```

time: 69.4 us -> 45.1 us (0.65)
  Pallas kernels: 68.9 us -> 44.9 us
    pallas_call x2, Pallas kernels: 68.9 us -> 44.9 us  [the longest x1 42.5 us: exchange(): pl.pallas_call(functools.partial(exchange_kernel, tokens), out_shape=pltp...]
where the time goes in v2:
time: 45.1 us; the launch traced here: 45 us
  Pallas kernels  44.9 us (100%)
    pallas_call x1, Pallas kernels, exchange(): pl.pallas_call(functools.partial(exchange_kernel, tokens), out_shape=pltp...  42.5 us
    pallas_call x1, Pallas kernels, store(): pl.pallas_call(store_kernel, out_shape=jax.ShapeDtypeStruct(update.shape,...  2.37 us

profile of v2, /device:TPU:0, one launch (start us, length us, event | category | flops | bytes accessed | tf_op | source)
XLA Modules:
  0.0 45.0 jit_solution(2667909609190816605)
XLA Ops:
  0.0 42.5 %exchange.1.src = bf16[1,5120,512]{2,1,0:T(8,128)(2,1)S(1)} custom-call(s32[1,52]{1,0:T(1,128)} %sweeps_hbm.1, bf16[1,384,8192]{2,1,0:T(8,128)(2,1)} %acts.1, bf16[1,384,5120]{2,1,0:T(8,128)(2,1)} %grads.1, bf16[384,5120]{1,0:T(8,128)(2,1)} %head.1, bf16[1,5120,512]{2,1,0:T(8,128)(2,1)} %weights.1), custom_call_target="tpu_custom_call" | custom-call | tf_op jit(solution)/shard_map/exchange/pallas_call | solution.py:377
  42.5 2.4 %store.1 = bf16[1,5120,512]{2,1,0:T(8,128)(2,1)} custom-call(bf16[1,5120,512]{2,1,0:T(8,128)(2,1)S(1)} %exchange.1.src), custom_call_target="tpu_custom_call" | custom-call | tf_op jit(solution)/shard_map/store/pallas_call | solution.py:408

commit v3 on v2

--- a/solution.py
+++ b/solution.py
@@ -112,10 +112,10 @@
 
 
 def exchange_kernel(
-    tokens, sweeps_hbm, acts, grads, head, weights, out, sweeps,
-    x_a, x_g, w, half, gs1, go1, gr1, gs2, gr2, gs3, gr3, gs4, gx0, gx1,
+    tokens, sweeps_hbm, acts, grads, head, weights, applied, inv_a, sweeps,
+    x_a, x_g, w, gs1, go1, gr1, gs2, gr2, gs3, gr3, gs4, gx0, gx1,
     own, r2, y3, y2, d_own, d_r2, d_y3, d_y2,
-    as1, ao1, ar1, as2, ar2, as3, ar3, as4, ar4, inv_a, load_sem, send_sem, recv_sem,
+    as1, ao1, ar1, as2, ar2, as3, ar3, as4, ar4, load_sem, send_sem, recv_sem,
 ):
     section = lax.axis_index("section")
     dp = lax.axis_index("dp")
@@ -151,32 +151,43 @@
         copy.start()
         return copy
 
-    g_chunk, a_chunk, w_chunk = x_g.shape[1] // 2, x_a.shape[1] // 2, w.shape[0] // 2
-    model_blocks, hidden_blocks = x_g.shape[1] // BLOCK, x_a.shape[1] // BLOCK
+    w_chunk = w.shape[0] // 2
+    hidden_blocks = x_a.shape[1] // BLOCK
+    o_core = 1 - core
+    g_groups = (o_core * 2 + n2, core * 2 + n1, o_core * 2 + b2, core * 2 + b1)
+    a_groups = ((o_core, n2, b1), (core, n1, b2), (o_core, b2, b1), (core, b1, b2))
 
     def load_g(i, src):
-        part = pl.ds(i * g_chunk, g_chunk)
+        part = pl.ds(pl.multiple_of(g_groups[i] * 5 * BLOCK, BLOCK), 5 * BLOCK)
         return pltpu.make_async_copy(src.at[:, part], x_g.at[:, part], load_sem.at[i])
 
-    def load_a(i):
-        part = pl.ds(i * a_chunk, a_chunk)
-        return pltpu.make_async_copy(acts.at[0, :, part], x_a.at[:, part], load_sem.at[2 + i])
+    def leaf(of_core, first, bit, u):
+        middle = lax.rem(first + bit, 2)
+        return (1 - x if u == 0 else x) * 8 + (jnp.where(of_core == 0, bit, first) * 2 + middle) * 2 + of_core
+
+    def load_a(i, b, u):
+        of_core, first, second = a_groups[i]
+        owner = leaf(of_core, first, second if b else 1 - second, u)
+        part = pl.ds(pl.multiple_of(owner * 2 * BLOCK, 2 * BLOCK), 2 * BLOCK)
+        return pltpu.make_async_copy(acts.at[0, :, part], x_a.at[:, part], load_sem.at[4 + i * 4 + b * 2 + u])
+
+    a_loads = [(b, u) for b in range(2) for u in range(2)]
 
     def load_w(i):
         part = pl.ds(i * w_chunk, w_chunk)
-        return pltpu.make_async_copy(weights.at[0, part, :], w.at[part, :], load_sem.at[4 + i])
+        return pltpu.make_async_copy(weights.at[0, part, :], w.at[part, :], load_sem.at[20 + i])
 
     @pl.when(section == 0)
     def _():
-        for i in range(2):
+        for i in range(4):
             load_g(i, head).start()
 
     @pl.when(section > 0)
     def _():
-        for i in range(2):
+        for i in range(4):
             load_g(i, grads.at[0]).start()
 
-    load_sweeps = pltpu.make_async_copy(sweeps_hbm, sweeps, load_sem.at[6])
+    load_sweeps = pltpu.make_async_copy(sweeps_hbm, sweeps, load_sem.at[22])
     load_sweeps.start()
     barrier = pltpu.get_barrier_semaphore()
     greeted = (p_core, p_y1, p_y2, p_x, p_straight, p_cross, (above, dp), (above, crossed))
@@ -191,51 +202,50 @@
     def place(k, bit):
         return (1 - bit) * 3 + k if k < 2 else 2 if k == 2 else bit * 3 + k - 3
 
-    def g_partials(dst, at, group, bit):
+    def g_partials(dst, at, i):
+        load_g(i, head).wait()
+        bit = (b1, b2)[i % 2]
         for k in range(5):
-            store_packed(dst, at + k, outer(x_g, group * 5 + place(k, bit)))
-
-    def a_partials(dst, at, of_core, first, second):
+            store_packed(dst, at + k, outer(x_g, g_groups[i] * 5 + place(k, bit)))
+
+    def a_partials(dst, at, i):
+        of_core, first, second = a_groups[i]
+        for b, u in a_loads:
+            load_a(i, b, u).wait()
+
         @pl.loop(0, 2)
         def _(e):
             bit = jnp.where(e == 0, 1 - second, second)
             for u in range(2):
-                owner = (1 - x if u == 0 else x) * 8
+                owner = leaf(of_core, first, bit, u)
                 for j in range(2):
-                    for_core_0 = owner + (bit * 2 + lax.rem(first + bit, 2)) * 2
-                    for_core_1 = owner + (first * 2 + lax.rem(first + bit, 2)) * 2 + 1
-                    block = jnp.where(of_core == 0, for_core_0, for_core_1) * 2 + j
-                    store_packed(dst, at + 4 * e + 2 * u + j, outer(x_a, block))
+                    store_packed(dst, at + 4 * e + 2 * u + j, outer(x_a, owner * 2 + j))
 
     def add_blocks(dst, di, size, a, ai, b, bi):
         @pl.loop(0, size)
         def _(i):
             add_packed(dst, di + i, a, ai + i, b, bi + i)
 
-    load_g(0, head).wait()
-    load_g(1, head).wait()
-    for i in range(2):
-        load_a(i).start()
-    o_core = 1 - core
-    g_partials(gs1, 0, o_core * 2 + n2, b1)
+    g_partials(gs1, 0, 0)
+    for i in range(4):
+        for b, u in a_loads:
+            load_a(i, b, u).start()
     pl.semaphore_wait(barrier, len(greeted))
     g_core = [send(gs1.at[pl.ds(0, 5)], gr1.at[pl.ds(0, 5)], p_core)]
-    g_partials(go1, 0, core * 2 + n1, b2)
+    g_partials(go1, 0, 1)
+    g_partials(gs1, 5, 2)
+    g_core.append(send(gs1.at[pl.ds(5, 5)], gr1.at[pl.ds(5, 5)], p_core))
     g_core[0].wait()
     g_y1 = []
     for k in range(5):
         add_packed(gs2, k, go1, k, gr1, k)
         g_y1.append(send(gs2.at[k], gr2.at[k], p_y1))
-    g_partials(gs1, 5, o_core * 2 + b2, b1)
-    g_core.append(send(gs1.at[pl.ds(5, 5)], gr1.at[pl.ds(5, 5)], p_core))
-    g_partials(go1, 5, core * 2 + b1, b2)
-    for i in range(2):
-        load_a(i).wait()
+    g_partials(go1, 5, 3)
+    a_partials(as1, 0, 0)
+    a_core = [send(as1.at[pl.ds(0, 8)], ar1.at[pl.ds(0, 8)], p_core)]
+    a_partials(ao1, 0, 1)
     for i in range(2):
         load_w(i).start()
-    a_partials(as1, 0, o_core, n2, b1)
-    a_core = [send(as1.at[pl.ds(0, 8)], ar1.at[pl.ds(0, 8)], p_core)]
-    a_partials(ao1, 0, core, n1, b2)
     g_core[1].wait()
     add_blocks(go1, 5, 5, go1, 5, gr1, 5)
     g_y2 = []
@@ -243,13 +253,17 @@
         g_y1[k].wait()
         add_packed(gs3, k, go1, 5 + k, gr2, k)
         g_y2.append(send(gs3.at[k], gr3.at[k], p_y2))
+    a_partials(as1, 8, 2)
+    a_core.append(send(as1.at[pl.ds(8, 8)], ar1.at[pl.ds(8, 8)], p_core))
     a_core[0].wait()
     a_y1 = []
-    for i in range(2):
+
+    def a_first(i):
         add_blocks(as2, 4 * i, 4, ao1, 4 * i, ar1, 4 * i)
         a_y1.append(send(as2.at[pl.ds(4 * i, 4)], ar2.at[pl.ds(4 * i, 4)], p_y1))
-    a_partials(as1, 8, o_core, b2, b1)
-    a_core.append(send(as1.at[pl.ds(8, 8)], ar1.at[pl.ds(8, 8)], p_core))
+
+    a_partials(ao1, 8, 3)
+    a_first(0)
     g_over = []
     for k in range(3):
         mine = (8, 9, 7)[k]
@@ -259,14 +273,12 @@
         add_packed(go1, mine, go1, mine, gr2, mine - 5)
         add_packed(gs4, k, go1, mine, gr3, k)
         g_over.append((send(gs4.at[k], gx0.at[k], p_straight), send(gs4.at[k], gx1.at[k], p_cross)))
-    a_partials(ao1, 8, core, b1, b2)
+    a_first(1)
     a_core[1].wait()
     add_blocks(ao1, 8, 8, ao1, 8, ar1, 8)
     a_y1[0].wait()
     add_blocks(as3, 0, 4, ao1, 8, ar2, 0)
     a_y2 = [send(as3.at[pl.ds(2 * i, 2)], ar3.at[pl.ds(2 * i, 2)], p_y2) for i in range(2)]
-    a_y1[1].wait()
-    add_blocks(ao1, 12, 4, ao1, 12, ar2, 4)
     load_sweeps.wait()
     row, column = iotas(BLOCK, BLOCK)
     damp = jnp.where(row == column, DAMPING, 0.0).astype(F32)
@@ -274,83 +286,89 @@
     here, there = core * 10, o_core * 10
     g_own, g_r2, g_own_core, g_y3_core = [], [], [], []
 
-    def g_invert(k):
-        g_over[k][0].wait()
-        g_over[k][1].wait()
-        factor = load_full_sum(gx0, k, gx1, k) * mean + damp
-        at = here + b1 * 5 + (b2 * 3 + k if k < 2 else 2)
-        store_packed(own, k, newton([factor], [sweeps[0, hidden_blocks + at]])[0])
-        if k < 2:
-            g_r2.append(send(own.at[k], r2.at[k], p_y2))
+    first = here + b1 * 5
+    at = (first + b2 * 3, first + b2 * 3 + 1, first + 2)
+
+    def g_invert(places):
+        for k in places:
+            for copy in g_over[k]:
+                copy.wait()
+        factors = [load_full_sum(gx0, k, gx1, k) * mean + damp for k in places]
+        for k, inverse in zip(places, newton(factors, [sweeps[0, hidden_blocks + at[k]] for k in places])):
+            store_packed(own, k, inverse)
+
+    def gather_first(k):
         g_own.append(send(own.at[k], y3.at[k], p_y1))
+
+    def gather_second(k):
+        g_r2.append(send(own.at[k], r2.at[k], p_y2))
+
+    def gather_core(k):
         g_own_core.append(send(own.at[k], d_own.at[k], p_core))
 
-    g_invert(0)
+    relayed, y2_core = [], []
+
+    def relay(k):
+        g_r2[k].wait()
+        relayed.append((send(r2.at[k], y2.at[k], p_y1), send(r2.at[k], d_r2.at[k], p_core)))
+
+    def pass_own(k):
+        g_own[k].wait()
+        g_y3_core.append(send(y3.at[k], d_y3.at[k], p_core))
+
+    def pass_y2(k):
+        relayed[k][0].wait()
+        y2_core.append(send(y2.at[k], d_y2.at[k], p_core))
+
+    def apply(src, i, block):
+        rows = pl.ds(pl.multiple_of(block * BLOCK, BLOCK), BLOCK)
+        inverse = load_full(src, i).astype(BF16)
+        applied[0, rows, :] = jnp.dot(inverse, w[rows, :], preferred_element_type=F32).astype(BF16)
+
+    def apply_own(src, group, bit):
+        for k in range(3):
+            apply(src, k, group + (bit * 3 + k if k < 2 else 2))
+
+    def apply_r2(src, group, bit):
+        for k in range(2):
+            apply(src, k, group + bit * 3 + k)
+
+    g_invert((0, 1))
+    gather_second(0)
+    gather_second(1)
+    gather_core(0)
+    gather_core(1)
+    a_y1[1].wait()
+    add_blocks(ao1, 12, 4, ao1, 12, ar2, 4)
     a_y2[0].wait()
     add_blocks(as4, 0, 2, ao1, 12, ar3, 0)
     a_x = send(as4, ar4, p_x)
     a_y2[1].wait()
     add_blocks(ao1, 14, 2, ao1, 14, ar3, 2)
-    g_invert(1)
-    g_invert(2)
+    gather_first(0)
+    g_invert((2,))
+    gather_core(2)
+    gather_first(1)
+    gather_first(2)
     for i in range(2):
         load_w(i).wait()
-    relayed, y2_core = [], []
-
-    def relay(k):
-        g_r2[k].wait()
-        relayed.append((send(r2.at[k], y2.at[k], p_y1), send(r2.at[k], d_r2.at[k], p_core)))
-
-    def pass_own(k):
-        g_own[k].wait()
-        g_y3_core.append(send(y3.at[k], d_y3.at[k], p_core))
-
-    def pass_y2(k):
-        relayed[k][0].wait()
-        y2_core.append(send(y2.at[k], d_y2.at[k], p_core))
-
+    apply_own(own, first, b2)
     relay(0)
     relay(1)
+    apply_r2(r2, first, n2)
+    for k in range(3):
+        g_own_core[k].wait()
+    apply_own(d_own, there + b2 * 5, b1)
+    for k in range(3):
+        pass_own(k)
     a_x.wait()
     factors = [load_full_sum(ao1, 14 + j, ar4, j) * mean + damp for j in range(2)]
     for j, inverse in enumerate(newton(factors, [sweeps[0, dp * 2 + j] for j in range(2)])):
         inv_a[j, :, :] = inverse.astype(BF16)
-    for k in range(3):
-        pass_own(k)
-
-    def halves(start, stop):
-        @pl.loop(start // 2, stop // 2)
-        def _(k):
-            rows = pl.ds(pl.multiple_of(k * 2 * BLOCK, 2 * BLOCK), 2 * BLOCK)
-            for j in range(2):
-                columns = slice(j * BLOCK, (j + 1) * BLOCK)
-                half[rows, columns] = jnp.dot(w[rows, columns], inv_a[j], preferred_element_type=F32).astype(BF16)
-
-    halves(0, 10)
     pass_y2(0)
+    apply_own(y3, here + n1 * 5, b2)
     pass_y2(1)
-    halves(10, model_blocks)
-
-    def apply(src, i, block):
-        rows = pl.ds(pl.multiple_of(block * BLOCK, BLOCK), BLOCK)
-        inverse = load_full(src, i).astype(BF16)
-        out[0, rows, :] = jnp.dot(inverse, half[rows, :], preferred_element_type=F32).astype(BF16)
-
-    def apply_own(src, group, bit):
-        for k in range(3):
-            apply(src, k, group + (bit * 3 + k if k < 2 else 2))
-
-    def apply_r2(src, group, bit):
-        for k in range(2):
-            apply(src, k, group + bit * 3 + k)
-
-    apply_own(own, here + b1 * 5, b2)
-    apply_r2(r2, here + b1 * 5, n2)
-    apply_own(y3, here + n1 * 5, b2)
     apply_r2(y2, here + n1 * 5, n2)
-    for k in range(3):
-        g_own_core[k].wait()
-    apply_own(d_own, there + b2 * 5, b1)
     for k in range(2):
         relayed[k][1].wait()
     apply_r2(d_r2, there + b2 * 5, n1)
@@ -376,18 +394,16 @@
     a_counts = (16, 16, 16, 8, 8, 4, 4, 2, 2)
     return pl.pallas_call(
         functools.partial(exchange_kernel, tokens),
-        out_shape=pltpu.VMEM(weights.shape, BF16),
+        out_shape=(pltpu.VMEM(weights.shape, BF16), pltpu.VMEM((2, BLOCK, BLOCK), BF16)),
         in_specs=[hbm] * 5,
-        out_specs=vmem,
+        out_specs=(vmem, vmem),
         scratch_shapes=[
             pltpu.SMEM(sweeps.shape, jnp.int32),
             pltpu.VMEM((rows, acts.shape[2]), BF16),
             pltpu.VMEM((rows, grads.shape[2]), BF16),
             pltpu.VMEM(weights.shape[1:], BF16),
-            pltpu.VMEM(weights.shape[1:], BF16),
             *[packed(n) for n in g_counts + gather_counts + a_counts],
-            pltpu.VMEM((2, BLOCK, BLOCK), BF16),
-            pltpu.SemaphoreType.DMA((7,)),
+            pltpu.SemaphoreType.DMA((23,)),
             pltpu.SemaphoreType.DMA((41,)),
             pltpu.SemaphoreType.DMA((41,)),
         ],
@@ -398,27 +414,41 @@
     )(*operands)
 
 
-def store_kernel(src, dst, sem):
-    copy = pltpu.make_async_copy(src, dst, sem)
-    copy.start()
-    copy.wait()
-
-
-def store(update):
+def finish_kernel(applied, inv_a, out, tiles, sems):
+    rows = 2 * BLOCK
+    copies = []
+    for i in range(tiles.shape[0] // rows):
+        part = pl.ds(i * rows, rows)
+        for j in range(2):
+            columns = slice(j * BLOCK, (j + 1) * BLOCK)
+            tiles[part, columns] = jnp.dot(
+                applied[0, part, columns], inv_a[j], preferred_element_type=F32
+            ).astype(BF16)
+        copies.append(pltpu.make_async_copy(tiles.at[part, :], out.at[0, part, :], sems.at[i]))
+        copies[-1].start()
+    for copy in copies:
+        copy.wait()
+
+
+def finish(applied, inv_a):
+    vmem = pl.BlockSpec(memory_space=pltpu.VMEM)
     return pl.pallas_call(
-        store_kernel,
-        out_shape=jax.ShapeDtypeStruct(update.shape, update.dtype),
-        in_specs=[pl.BlockSpec(memory_space=pltpu.VMEM)],
+        finish_kernel,
+        out_shape=jax.ShapeDtypeStruct(applied.shape, applied.dtype),
+        in_specs=[vmem, vmem],
         out_specs=pl.BlockSpec(memory_space=pltpu.HBM),
-        scratch_shapes=[pltpu.SemaphoreType.DMA],
-        compiler_params=pltpu.CompilerParams(vmem_limit_bytes=1024 * 1024),
-        name="store",
-    )(update)
+        scratch_shapes=[
+            pltpu.VMEM(applied.shape[1:], applied.dtype),
+            pltpu.SemaphoreType.DMA((applied.shape[1] // (2 * BLOCK),)),
+        ],
+        compiler_params=pltpu.CompilerParams(vmem_limit_bytes=12 * 1024 * 1024),
+        name="finish",
+    )(applied, inv_a)
 
 
 def on_device(acts, input_grads, head_grads, weight_grad, sweeps):
     tokens = acts.shape[1] * lax.axis_size("dp")
-    return store(exchange(tokens, sweeps, acts, input_grads, head_grads, weight_grad))
+    return finish(*exchange(tokens, sweeps, acts, input_grads, head_grads, weight_grad))
 
 
 def solution(mesh):

time: 45.1 us -> 42.1 us (0.933)
  the two profiles are of different devices: /device:TPU:0 before, /device:TPU:1 now
where the time goes in v3:
time: 42.1 us; the launch traced here: 42 us
  Pallas kernels  41.8 us (99%)
    pallas_call x1, Pallas kernels, exchange(): pl.pallas_call(functools.partial(exchange_kernel, tokens), out_shape=(plt...  39.1 us
    pallas_call x1, Pallas kernels, finish(): pl.pallas_call(finish_kernel, out_shape=jax.ShapeDtypeStruct(applied.shap...  2.72 us

profile of v3, /device:TPU:1, one launch (start us, length us, event | category | flops | bytes accessed | tf_op | source)
XLA Modules:
  0.0 42.0 jit_solution(767435759171424729)
XLA Ops:
  0.0 39.1 %exchange.1 = (bf16[1,5120,512]{2,1,0:T(8,128)(2,1)S(1)}, bf16[2,256,256]{2,1,0:T(8,128)(2,1)S(1)}) custom-call(s32[1,52]{1,0:T(1,128)} %sweeps_hbm.1, bf16[1,384,8192]{2,1,0:T(8,128)(2,1)} %acts.1, bf16[1,384,5120]{2,1,0:T(8,128)(2,1)} %grads.1, bf16[384,5120]{1,0:T(8,128)(2,1)} %head.1, bf16[1,5120,512]{2,1,0:T(8,128)(2,1)} %weights.1), custom_call_target="tpu_custom_call" | custom-call | tf_op jit(solution)/shard_map/exchange/pallas_call | solution.py:395
  39.1 2.7 %finish.1 = bf16[1,5120,512]{2,1,0:T(8,128)(2,1)} custom-call(bf16[1,5120,512]{2,1,0:T(8,128)(2,1)S(1)} %get-tuple-element.7.applied, bf16[2,256,256]{2,1,0:T(8,128)(2,1)S(1)} %get-tuple-element.8.inv_a), custom_call_target="tpu_custom_call" | custom-call | tf_op jit(solution)/shard_map/finish/pallas_call | solution.py:435

commit v4 on v3

--- a/solution.py
+++ b/solution.py
@@ -343,18 +343,18 @@
     a_y2[0].wait()
     add_blocks(as4, 0, 2, ao1, 12, ar3, 0)
     a_x = send(as4, ar4, p_x)
-    a_y2[1].wait()
-    add_blocks(ao1, 14, 2, ao1, 14, ar3, 2)
     gather_first(0)
     g_invert((2,))
     gather_core(2)
     gather_first(1)
     gather_first(2)
+    a_y2[1].wait()
+    add_blocks(ao1, 14, 2, ao1, 14, ar3, 2)
     for i in range(2):
         load_w(i).wait()
-    apply_own(own, first, b2)
     relay(0)
     relay(1)
+    apply_own(own, first, b2)
     apply_r2(r2, first, n2)
     for k in range(3):
         g_own_core[k].wait()

time: 42.1 us -> 40.6 us (0.964)
  Pallas kernels: 41.8 us -> 40.3 us
    pallas_call x1, Pallas kernels: 39.1 us -> 37.6 us  [exchange(): pl.pallas_call(functools.partial(exchange_kernel, tokens), out_shape=(plt...]
where the time goes in v4:
time: 40.6 us; the launch traced here: 40.5 us
  Pallas kernels  40.3 us (99%)
    pallas_call x1, Pallas kernels, exchange(): pl.pallas_call(functools.partial(exchange_kernel, tokens), out_shape=(plt...  37.6 us
    pallas_call x1, Pallas kernels, finish(): pl.pallas_call(finish_kernel, out_shape=jax.ShapeDtypeStruct(applied.shap...  2.72 us

profile of v4, /device:TPU:1, one launch (start us, length us, event | category | flops | bytes accessed | tf_op | source)
XLA Modules:
  0.0 40.5 jit_solution(3404116825645928149)
XLA Ops:
  0.0 37.6 %exchange.1 = (bf16[1,5120,512]{2,1,0:T(8,128)(2,1)S(1)}, bf16[2,256,256]{2,1,0:T(8,128)(2,1)S(1)}) custom-call(s32[1,52]{1,0:T(1,128)} %sweeps_hbm.1, bf16[1,384,8192]{2,1,0:T(8,128)(2,1)} %acts.1, bf16[1,384,5120]{2,1,0:T(8,128)(2,1)} %grads.1, bf16[384,5120]{1,0:T(8,128)(2,1)} %head.1, bf16[1,5120,512]{2,1,0:T(8,128)(2,1)} %weights.1), custom_call_target="tpu_custom_call" | custom-call | tf_op jit(solution)/shard_map/exchange/pallas_call | solution.py:395
  37.6 2.7 %finish.1 = bf16[1,5120,512]{2,1,0:T(8,128)(2,1)} custom-call(bf16[1,5120,512]{2,1,0:T(8,128)(2,1)S(1)} %get-tuple-element.7.applied, bf16[2,256,256]{2,1,0:T(8,128)(2,1)S(1)} %get-tuple-element.8.inv_a), custom_call_target="tpu_custom_call" | custom-call | tf_op jit(solution)/shard_map/finish/pallas_call | solution.py:435
